TPU v7x, 8 devices: a whole 2x2x1 slice. The times are simulated.
8 devices in a mesh: data: 1 (over z), cp: 8 (over y, x, core).
Axes of the slice: x: 2, y: 2, z: 1, core: 2. Of those that a mesh axis runs over, the one named last changes fastest.
Arguments:
- x_tokens: bfloat16 [16, 2048, 5120], P('data', 'cp')
- positions: int32 [16, 2048], P('data', 'cp')
- w_query: bfloat16 [5120, 5120], replicated
- w_key: bfloat16 [5120, 1024], replicated
- w_value: bfloat16 [5120, 1024], replicated
- w_out: bfloat16 [5120, 5120], replicated
Outputs:
- output: bfloat16 [16, 2048, 5120], P('data', 'cp')
All inputs are finite; a program needn't handle non-finite values.
Results may differ from a plain program's by a relative error of at most 0.00471873.
Values are sent between devices in bfloat16 or wider.
A program may use at most 1 GiB of HBM per device.

v0:
```python
import jax
import jax.numpy as jnp
from jax import lax
from jax.sharding import PartitionSpec as P

HEAD_DIM = 128
ROPE_BASE = 500000
MASK_FILL = -1e30


def apply_rope(head_vecs, positions):
    half_dim = HEAD_DIM // 2
    inv_freq = 1.0 / (ROPE_BASE ** (jnp.arange(0, HEAD_DIM, 2, dtype=jnp.float32) / HEAD_DIM))
    angles = positions.astype(jnp.float32)[:, :, None] * inv_freq
    tab_shape = angles.shape[:2] + (1,) * (head_vecs.ndim - 3) + (half_dim,)
    cosine = jnp.cos(angles).reshape(tab_shape)
    sine_tab = jnp.sin(angles).reshape(tab_shape)
    lower_half = head_vecs[..., :half_dim].astype(jnp.float32)
    upper_half = head_vecs[..., half_dim:].astype(jnp.float32)
    rotated = jnp.concatenate([lower_half * cosine - upper_half * sine_tab, upper_half * cosine + lower_half * sine_tab], axis=-1)
    return rotated.astype(jnp.bfloat16)


def project_qkv(x_rows, pos_rows, w_query, w_key, w_value):
    batch_rows, tok_rows, model_dim = x_rows.shape
    kv_heads = w_key.shape[1] // HEAD_DIM
    group_size = w_query.shape[1] // w_key.shape[1]
    flat_x = x_rows.reshape(batch_rows * tok_rows, model_dim)
    q_proj = jnp.dot(flat_x, w_query, preferred_element_type=jnp.float32).astype(jnp.bfloat16)
    k_proj = jnp.dot(flat_x, w_key, preferred_element_type=jnp.float32).astype(jnp.bfloat16)
    v_proj = jnp.dot(flat_x, w_value, preferred_element_type=jnp.float32).astype(jnp.bfloat16)
    q_rot = apply_rope(q_proj.reshape(batch_rows, tok_rows, kv_heads, group_size, HEAD_DIM), pos_rows)
    k_rot = apply_rope(k_proj.reshape(batch_rows, tok_rows, kv_heads, HEAD_DIM), pos_rows)
    return q_rot, k_rot, v_proj.reshape(batch_rows, tok_rows, kv_heads, HEAD_DIM)


def empty_state(q_rot):
    batch_rows, tok_rows, kv_heads, group_size, _ = q_rot.shape
    state_shape = (batch_rows, kv_heads, group_size, tok_rows)
    return (jnp.full(state_shape, MASK_FILL, jnp.float32), jnp.zeros(state_shape, jnp.float32), jnp.zeros(state_shape + (HEAD_DIM,), jnp.float32))


def attend_block(q_rows, k_blk, v_blk, carry_state, allowed):
    m_run, l_run, acc_run = carry_state
    scores = jnp.einsum('bqhgd,bkhd->bhgqk', q_rows, k_blk, preferred_element_type=jnp.float32) * (HEAD_DIM ** -0.5)
    if allowed is not None:
        scores = jnp.where(allowed, scores, MASK_FILL)
    m_new = jnp.maximum(m_run, jnp.max(scores, axis=-1))
    exp_w = jnp.exp(scores - m_new[..., None])
    if allowed is not None:
        exp_w = jnp.where(allowed, exp_w, 0.0)
    rescale = jnp.exp(m_run - m_new)
    l_new = rescale * l_run + jnp.sum(exp_w, axis=-1)
    pv_part = jnp.einsum('bhgqk,bkhd->bhgqd', exp_w.astype(jnp.bfloat16), v_blk, preferred_element_type=jnp.float32)
    return m_new, l_new, rescale[..., None] * acc_run + pv_part


def attend_remote(q_loc, k_recv, v_recv, carry_state, src_before):
    half_len = q_loc.shape[1] // 2

    def keys_before(state_in):
        return attend_block(q_loc, k_recv[:, :half_len], v_recv[:, :half_len], state_in, None)

    def keys_after(state_in):
        m_run, l_run, acc_run = state_in
        tail_state = (m_run[..., half_len:], l_run[..., half_len:], acc_run[..., half_len:, :])
        m_new, l_new, acc_new = attend_block(q_loc[:, half_len:], k_recv, v_recv, tail_state, None)
        return (jnp.concatenate([m_run[..., :half_len], m_new], axis=-1), jnp.concatenate([l_run[..., :half_len], l_new], axis=-1), jnp.concatenate([acc_run[..., :half_len, :], acc_new], axis=-2))

    return lax.cond(src_before, keys_before, keys_after, carry_state)


def output_proj(x_rows, final_state, w_out):
    _, l_run, acc_run = final_state
    kv_heads, group_size = acc_run.shape[1], acc_run.shape[2]
    normed = (acc_run / l_run[..., None]).astype(jnp.bfloat16)
    w_heads = w_out.reshape(kv_heads, group_size, HEAD_DIM, w_out.shape[1])
    out_proj = jnp.einsum('bhgqd,hgde->bqe', normed, w_heads, preferred_element_type=jnp.float32)
    return (x_rows.astype(jnp.float32) + out_proj).astype(jnp.bfloat16)


def solution(mesh):
    cp_size = mesh.shape['cp']
    row_spec = P('data', 'cp', None)
    pos_spec = P('data', 'cp')
    rep_spec = P(None, None)
    shift_pairs = [(src_dev, (src_dev + 1) % cp_size) for src_dev in range(cp_size)]

    def local_block(x_loc, pos_loc, w_query, w_key, w_value, w_out):
        my_idx = lax.axis_index('cp')
        q_loc, k_loc, v_loc = project_qkv(x_loc, pos_loc, w_query, w_key, w_value)
        allowed = (pos_loc[:, None, :] <= pos_loc[:, :, None])[:, None, None]
        diag_state = attend_block(q_loc, k_loc, v_loc, empty_state(q_loc), allowed)

        def shift_step(step_idx, loop_in):
            k_cur, v_cur, carry_state = loop_in
            k_next = lax.ppermute(k_cur, 'cp', shift_pairs)
            v_next = lax.ppermute(v_cur, 'cp', shift_pairs)
            src_idx = (my_idx - step_idx) % cp_size
            return k_next, v_next, attend_remote(q_loc, k_next, v_next, carry_state, src_idx < my_idx)

        _, _, final_state = lax.fori_loop(1, cp_size, shift_step, (k_loc, v_loc, diag_state))
        return output_proj(x_loc, final_state, w_out)

    return jax.shard_map(local_block, mesh=mesh, in_specs=(row_spec, pos_spec, rep_spec, rep_spec, rep_spec, rep_spec), out_specs=row_spec, check_vma=False)
```

profile of v0, /device:TPU:0, one launch (start us, length us, event | category | flops | bytes accessed | tf_op | source)
XLA Modules:
  0.0 4165.4 jit_solution(4382964262801094028)
XLA Ops:
  0.0 227.9 %convolution_convert_fusion = bf16[4096,5120]{1,0:T(8,128)(2,1)} fusion(bf16[4096,5120]{1,0:T(8,128)(2,1)} %bitcast.128, bf16[5120,5120]{1,0:T(8,128)(2,1)} %param.12), kind=kOutput, calls=%fused_computation.62 | convolution fusion | flops 214769336320 | bytes 136314880 | tf_op jit(solution)/shard_map/dot_general | solution.py:29
  227.9 92.7 %reshape.60 = bf16[16,256,8,5,128]{4,3,2,1,0:T(8,128)(2,1)} reshape(bf16[4096,5120]{1,0:T(8,128)(2,1)} %convolution_convert_fusion) | data formatting | bytes 83886080 | tf_op jit(solution)/shard_map/reshape | solution.py:32
  320.5 87.4 %fusion.58 = (bf16[16,256,8,5,64]{4,3,2,1,0:T(8,128)(2,1)}, bf16[16,256,8,5,64]{4,3,2,1,0:T(8,128)(2,1)}) fusion(bf16[16,256,8,5,128]{4,3,2,1,0:T(8,128)(2,1)} %reshape.60), kind=kLoop, calls=%fused_computation.88 | loop fusion | bytes 83886080 | tf_op jit(solution)/shard_map/slice | solution.py:18
  416.6 186.3 %fusion.33 = (bf16[16,256,8,5,64]{4,1,3,2,0:T(8,128)(2,1)}, bf16[16,256,8,5,64]{4,1,3,2,0:T(8,128)(2,1)}) fusion(f32[16,256,64]{2,1,0:T(8,128)} %get-tuple-element.316, f32[16,256,64]{2,1,0:T(8,128)S(1)} %get-tuple-element.315, bf16[16,256,8,5,64]{4,3,2,1,0:T(8,128)(2,1)} %get-tuple-element.308, bf16[16,256,8,5,64]{4,3,2,1,0:T(8,128)(2,1)} %get-tuple-element.307), kind=kLoop, calls=%fused_computation.47 | loop fusion | flops 104857600 | bytes 85983232 | tf_op jit(solution)/shard_map/convert
  730.7 73.9 %fusion.29 = (f32[16,8,5,256]{3,2,1,0:T(8,128)S(1)}, f32[16,8,256,256,5]{3,2,4,1,0:T(8,128)}) fusion(pred[16,256,256]{1,2,0:T(8,128)(4,1)S(1)} %broadcast_compare_fusion, bf16[16,256,8,5,128]{4,1,3,2,0:T(8,128)(2,1)} %pad_maximum_fusion.3, bf16[16,256,8,128]{3,1,2,0:T(8,128)(2,1)} %pad_maximum_fusion.4), kind=kOutput, calls=%fused_computation.39 | convolution fusion | flops 10863083520 | bytes 219807744 | tf_op jit(solution)/shard_map/bqhgd,bkhd->bhgqk/dot_general | solution.py:45
  924.7 98.8 %broadcast_add_fusion = f32[16,8,5,256,128]{4,3,2,1,0:T(8,128)} fusion(f32[16,8,5,256]{3,2,1,0:T(8,128)S(1)} %get-tuple-element.313, f32[16,8,256,256,5]{3,2,4,1,0:T(8,128)} %get-tuple-element.318, f32[16,8,5,256]{3,2,1,0:T(8,128)S(1)} %broadcast_maximum_fusion, pred[16,256,256]{1,2,0:T(8,128)(4,1)S(1)} %broadcast_compare_fusion, ...), kind=kOutput, calls=%fused_computation.61 | convolution fusion | flops 10968104960 | bytes 262406144 | tf_op jit(solution)/shard_map/bhgqk,bkhd->bhgqd/dot_general | solution.py:54
  1032.6 2880.9 %while.23 = (s32[]{:T(128)}, bf16[16,256,8,128]{3,1,2,0:T(8,128)(2,1)}, bf16[16,256,8,128]{3,1,2,0:T(8,128)(2,1)}, f32[16,8,5,256]{3,2,1,0:T(8,128)}, f32[16,8,5...) while((s32[]{:T(128)}, ...), condition=%wide.region_9.10_spmd, body=%wide.region_2.9_spmd.sunk | while | flops 10947624960 | bytes 741999104 | solution.py:102
  1036.5 91.4 %collective-permute-done = bf16[16,256,8,128]{3,1,2,0:T(8,128)(2,1)} collective-permute-done((bf16[16,256,8,128]{3,1,2,0:T(8,128)(2,1)}, bf16[16,256,8,128]{3,1,2,0:T(8,128)(2,1)}, u32[]{:S(2)}, u32[]{:S(2)}) %collective-permute-start) | collective-permute-done | bytes 8388640 | tf_op jit(solution)/shard_map/while/body/eval_jaxpr/ppermute | solution.py:97
  1127.9 89.9 %collective-permute-done.1 = bf16[16,256,8,128]{3,1,2,0:T(8,128)(2,1)} collective-permute-done((bf16[16,256,8,128]{3,1,2,0:T(8,128)(2,1)}, bf16[16,256,8,128]{3,1,2,0:T(8,128)(2,1)}, u32[]{:S(2)}, u32[]{:S(2)}) %collective-permute-start.1) | collective-permute-done | bytes 8388640 | tf_op jit(solution)/shard_map/while/body/eval_jaxpr/ppermute | solution.py:98
  1217.8 209.7 %conditional.2 = (f32[16,8,5,256]{3,2,1,0:T(8,128)}, f32[16,8,5,256]{3,2,1,0:T(8,128)S(1)}, f32[16,8,5,256,128]{4,3,2,1,0:T(8,128)}) conditional(s32[]{:T(128)} %convert_element_type.130, (f32[16,8,5,256]{3,2,1,0:T(8,128)}, bf16[16,256,8,5,128]{4,1,3,2,0:T(8,128)(2,1)}, bf16[16,256,8,128]{3,1,2,0:T(8,128)(2,1)}, f32[16,8,5,256]{3,2,1,0:T(8,128)S(1)}, ...), branch_computations={%region_3.5_spmd, %region_6.8_spmd} | conditional | flops 10947624960 | bytes 640024704 | solution.py:70
  1445.5 93.8 %collective-permute-done = bf16[16,256,8,128]{3,1,2,0:T(8,128)(2,1)} collective-permute-done((bf16[16,256,8,128]{3,1,2,0:T(8,128)(2,1)}, bf16[16,256,8,128]{3,1,2,0:T(8,128)(2,1)}, u32[]{:S(2)}, u32[]{:S(2)}) %collective-permute-start) | collective-permute-done | bytes 8388640 | tf_op jit(solution)/shard_map/while/body/eval_jaxpr/ppermute | solution.py:97
  1539.2 89.9 %collective-permute-done.1 = bf16[16,256,8,128]{3,1,2,0:T(8,128)(2,1)} collective-permute-done((bf16[16,256,8,128]{3,1,2,0:T(8,128)(2,1)}, bf16[16,256,8,128]{3,1,2,0:T(8,128)(2,1)}, u32[]{:S(2)}, u32[]{:S(2)}) %collective-permute-start.1) | collective-permute-done | bytes 8388640 | tf_op jit(solution)/shard_map/while/body/eval_jaxpr/ppermute | solution.py:98
  1629.1 209.7 %conditional.2 = (f32[16,8,5,256]{3,2,1,0:T(8,128)}, f32[16,8,5,256]{3,2,1,0:T(8,128)S(1)}, f32[16,8,5,256,128]{4,3,2,1,0:T(8,128)}) conditional(s32[]{:T(128)} %convert_element_type.130, (f32[16,8,5,256]{3,2,1,0:T(8,128)}, bf16[16,256,8,5,128]{4,1,3,2,0:T(8,128)(2,1)}, bf16[16,256,8,128]{3,1,2,0:T(8,128)(2,1)}, f32[16,8,5,256]{3,2,1,0:T(8,128)S(1)}, ...), branch_computations={%region_3.5_spmd, %region_6.8_spmd} | conditional | flops 10947624960 | bytes 640024704 | solution.py:70
  1856.8 93.8 %collective-permute-done = bf16[16,256,8,128]{3,1,2,0:T(8,128)(2,1)} collective-permute-done((bf16[16,256,8,128]{3,1,2,0:T(8,128)(2,1)}, bf16[16,256,8,128]{3,1,2,0:T(8,128)(2,1)}, u32[]{:S(2)}, u32[]{:S(2)}) %collective-permute-start) | collective-permute-done | bytes 8388640 | tf_op jit(solution)/shard_map/while/body/eval_jaxpr/ppermute | solution.py:97
  1950.6 89.9 %collective-permute-done.1 = bf16[16,256,8,128]{3,1,2,0:T(8,128)(2,1)} collective-permute-done((bf16[16,256,8,128]{3,1,2,0:T(8,128)(2,1)}, bf16[16,256,8,128]{3,1,2,0:T(8,128)(2,1)}, u32[]{:S(2)}, u32[]{:S(2)}) %collective-permute-start.1) | collective-permute-done | bytes 8388640 | tf_op jit(solution)/shard_map/while/body/eval_jaxpr/ppermute | solution.py:98
  2040.4 209.7 %conditional.2 = (f32[16,8,5,256]{3,2,1,0:T(8,128)}, f32[16,8,5,256]{3,2,1,0:T(8,128)S(1)}, f32[16,8,5,256,128]{4,3,2,1,0:T(8,128)}) conditional(s32[]{:T(128)} %convert_element_type.130, (f32[16,8,5,256]{3,2,1,0:T(8,128)}, bf16[16,256,8,5,128]{4,1,3,2,0:T(8,128)(2,1)}, bf16[16,256,8,128]{3,1,2,0:T(8,128)(2,1)}, f32[16,8,5,256]{3,2,1,0:T(8,128)S(1)}, ...), branch_computations={%region_3.5_spmd, %region_6.8_spmd} | conditional | flops 10947624960 | bytes 640024704 | solution.py:70
  2108.0 57.6 %multiply_add_fusion = f32[16,8,5,128,128]{4,3,2,1,0:T(8,128)} fusion(f32[16,8,5,256,128]{4,3,2,1,0:T(8,128)} %get-tuple-element.237, f32[16,8,5,128]{3,2,1,0:T(8,128)S(1)} %get-tuple-element.294, f32[16,8,256,128,5]{3,2,4,1,0:T(8,128)} %get-tuple-element.300, f32[16,8,5,128]{3,2,1,0:T(8,128)S(1)} %slice_maximum_fusion, ...), kind=kOutput, calls=%fused_computation.7 | convolution fusion | flops 5452595200 | bytes 176816128 | tf_op jit(solution)/shard_map/while/body/eval_jaxpr/cond/branch_0_fun/bhgqk,bkhd->bhgqd/dot_general | solution.py:54
  2268.1 93.8 %collective-permute-done = bf16[16,256,8,128]{3,1,2,0:T(8,128)(2,1)} collective-permute-done((bf16[16,256,8,128]{3,1,2,0:T(8,128)(2,1)}, bf16[16,256,8,128]{3,1,2,0:T(8,128)(2,1)}, u32[]{:S(2)}, u32[]{:S(2)}) %collective-permute-start) | collective-permute-done | bytes 8388640 | tf_op jit(solution)/shard_map/while/body/eval_jaxpr/ppermute | solution.py:97
  2361.9 89.9 %collective-permute-done.1 = bf16[16,256,8,128]{3,1,2,0:T(8,128)(2,1)} collective-permute-done((bf16[16,256,8,128]{3,1,2,0:T(8,128)(2,1)}, bf16[16,256,8,128]{3,1,2,0:T(8,128)(2,1)}, u32[]{:S(2)}, u32[]{:S(2)}) %collective-permute-start.1) | collective-permute-done | bytes 8388640 | tf_op jit(solution)/shard_map/while/body/eval_jaxpr/ppermute | solution.py:98
  2451.8 209.7 %conditional.2 = (f32[16,8,5,256]{3,2,1,0:T(8,128)}, f32[16,8,5,256]{3,2,1,0:T(8,128)S(1)}, f32[16,8,5,256,128]{4,3,2,1,0:T(8,128)}) conditional(s32[]{:T(128)} %convert_element_type.130, (f32[16,8,5,256]{3,2,1,0:T(8,128)}, bf16[16,256,8,5,128]{4,1,3,2,0:T(8,128)(2,1)}, bf16[16,256,8,128]{3,1,2,0:T(8,128)(2,1)}, f32[16,8,5,256]{3,2,1,0:T(8,128)S(1)}, ...), branch_computations={%region_3.5_spmd, %region_6.8_spmd} | conditional | flops 10947624960 | bytes 640024704 | solution.py:70
  2519.3 57.6 %multiply_add_fusion = f32[16,8,5,128,128]{4,3,2,1,0:T(8,128)} fusion(f32[16,8,5,256,128]{4,3,2,1,0:T(8,128)} %get-tuple-element.237, f32[16,8,5,128]{3,2,1,0:T(8,128)S(1)} %get-tuple-element.294, f32[16,8,256,128,5]{3,2,4,1,0:T(8,128)} %get-tuple-element.300, f32[16,8,5,128]{3,2,1,0:T(8,128)S(1)} %slice_maximum_fusion, ...), kind=kOutput, calls=%fused_computation.7 | convolution fusion | flops 5452595200 | bytes 176816128 | tf_op jit(solution)/shard_map/while/body/eval_jaxpr/cond/branch_0_fun/bhgqk,bkhd->bhgqd/dot_general | solution.py:54
  2679.4 93.8 %collective-permute-done = bf16[16,256,8,128]{3,1,2,0:T(8,128)(2,1)} collective-permute-done((bf16[16,256,8,128]{3,1,2,0:T(8,128)(2,1)}, bf16[16,256,8,128]{3,1,2,0:T(8,128)(2,1)}, u32[]{:S(2)}, u32[]{:S(2)}) %collective-permute-start) | collective-permute-done | bytes 8388640 | tf_op jit(solution)/shard_map/while/body/eval_jaxpr/ppermute | solution.py:97
  2773.2 89.9 %collective-permute-done.1 = bf16[16,256,8,128]{3,1,2,0:T(8,128)(2,1)} collective-permute-done((bf16[16,256,8,128]{3,1,2,0:T(8,128)(2,1)}, bf16[16,256,8,128]{3,1,2,0:T(8,128)(2,1)}, u32[]{:S(2)}, u32[]{:S(2)}) %collective-permute-start.1) | collective-permute-done | bytes 8388640 | tf_op jit(solution)/shard_map/while/body/eval_jaxpr/ppermute | solution.py:98
  2863.1 209.7 %conditional.2 = (f32[16,8,5,256]{3,2,1,0:T(8,128)}, f32[16,8,5,256]{3,2,1,0:T(8,128)S(1)}, f32[16,8,5,256,128]{4,3,2,1,0:T(8,128)}) conditional(s32[]{:T(128)} %convert_element_type.130, (f32[16,8,5,256]{3,2,1,0:T(8,128)}, bf16[16,256,8,5,128]{4,1,3,2,0:T(8,128)(2,1)}, bf16[16,256,8,128]{3,1,2,0:T(8,128)(2,1)}, f32[16,8,5,256]{3,2,1,0:T(8,128)S(1)}, ...), branch_computations={%region_3.5_spmd, %region_6.8_spmd} | conditional | flops 10947624960 | bytes 640024704 | solution.py:70
  3090.8 93.8 %collective-permute-done = bf16[16,256,8,128]{3,1,2,0:T(8,128)(2,1)} collective-permute-done((bf16[16,256,8,128]{3,1,2,0:T(8,128)(2,1)}, bf16[16,256,8,128]{3,1,2,0:T(8,128)(2,1)}, u32[]{:S(2)}, u32[]{:S(2)}) %collective-permute-start) | collective-permute-done | bytes 8388640 | tf_op jit(solution)/shard_map/while/body/eval_jaxpr/ppermute | solution.py:97
  3184.5 89.9 %collective-permute-done.1 = bf16[16,256,8,128]{3,1,2,0:T(8,128)(2,1)} collective-permute-done((bf16[16,256,8,128]{3,1,2,0:T(8,128)(2,1)}, bf16[16,256,8,128]{3,1,2,0:T(8,128)(2,1)}, u32[]{:S(2)}, u32[]{:S(2)}) %collective-permute-start.1) | collective-permute-done | bytes 8388640 | tf_op jit(solution)/shard_map/while/body/eval_jaxpr/ppermute | solution.py:98
  3274.4 209.7 %conditional.2 = (f32[16,8,5,256]{3,2,1,0:T(8,128)}, f32[16,8,5,256]{3,2,1,0:T(8,128)S(1)}, f32[16,8,5,256,128]{4,3,2,1,0:T(8,128)}) conditional(s32[]{:T(128)} %convert_element_type.130, (f32[16,8,5,256]{3,2,1,0:T(8,128)}, bf16[16,256,8,5,128]{4,1,3,2,0:T(8,128)(2,1)}, bf16[16,256,8,128]{3,1,2,0:T(8,128)(2,1)}, f32[16,8,5,256]{3,2,1,0:T(8,128)S(1)}, ...), branch_computations={%region_3.5_spmd, %region_6.8_spmd} | conditional | flops 10947624960 | bytes 640024704 | solution.py:70
  3502.1 93.8 %collective-permute-done = bf16[16,256,8,128]{3,1,2,0:T(8,128)(2,1)} collective-permute-done((bf16[16,256,8,128]{3,1,2,0:T(8,128)(2,1)}, bf16[16,256,8,128]{3,1,2,0:T(8,128)(2,1)}, u32[]{:S(2)}, u32[]{:S(2)}) %collective-permute-start) | collective-permute-done | bytes 8388640 | tf_op jit(solution)/shard_map/while/body/eval_jaxpr/ppermute | solution.py:97
  3595.8 89.9 %collective-permute-done.1 = bf16[16,256,8,128]{3,1,2,0:T(8,128)(2,1)} collective-permute-done((bf16[16,256,8,128]{3,1,2,0:T(8,128)(2,1)}, bf16[16,256,8,128]{3,1,2,0:T(8,128)(2,1)}, u32[]{:S(2)}, u32[]{:S(2)}) %collective-permute-start.1) | collective-permute-done | bytes 8388640 | tf_op jit(solution)/shard_map/while/body/eval_jaxpr/ppermute | solution.py:98
  3685.7 209.7 %conditional.2 = (f32[16,8,5,256]{3,2,1,0:T(8,128)}, f32[16,8,5,256]{3,2,1,0:T(8,128)S(1)}, f32[16,8,5,256,128]{4,3,2,1,0:T(8,128)}) conditional(s32[]{:T(128)} %convert_element_type.130, (f32[16,8,5,256]{3,2,1,0:T(8,128)}, bf16[16,256,8,5,128]{4,1,3,2,0:T(8,128)(2,1)}, bf16[16,256,8,128]{3,1,2,0:T(8,128)(2,1)}, f32[16,8,5,256]{3,2,1,0:T(8,128)S(1)}, ...), branch_computations={%region_3.5_spmd, %region_6.8_spmd} | conditional | flops 10947624960 | bytes 640024704 | solution.py:70
  3753.3 57.6 %multiply_add_fusion = f32[16,8,5,128,128]{4,3,2,1,0:T(8,128)} fusion(f32[16,8,5,256,128]{4,3,2,1,0:T(8,128)} %get-tuple-element.237, f32[16,8,5,128]{3,2,1,0:T(8,128)S(1)} %get-tuple-element.294, f32[16,8,256,128,5]{3,2,4,1,0:T(8,128)} %get-tuple-element.300, f32[16,8,5,128]{3,2,1,0:T(8,128)S(1)} %slice_maximum_fusion, ...), kind=kOutput, calls=%fused_computation.7 | convolution fusion | flops 5452595200 | bytes 176816128 | tf_op jit(solution)/shard_map/while/body/eval_jaxpr/cond/branch_0_fun/bhgqk,bkhd->bhgqd/dot_general | solution.py:54
  3913.5 251.7 %fusion.38 = bf16[16,256,5120]{2,1,0:T(8,128)(2,1)} fusion(bf16[16,256,5120]{2,1,0:T(8,128)(2,1)} %param.10, bf16[8,5,128,5120,1]{3,2,1,0,4:T(8,128)(2,1)} %bitcast.127, f32[16,8,5,256,128]{4,3,2,1,0:T(8,128)} %get-tuple-element.259, f32[16,8,5,256]{3,2,1,0:T(8,128)S(1)} %get-tuple-element.260), kind=kOutput, calls=%fused_computation.52 | convolution fusion | flops 214853222400 | bytes 220856320 | tf_op jit(solution)/shard_map/bhgqd,hgde->bqe/dot_general | solution.py:78
  (171 shorter events, 1689.9 us)
Async XLA Ops:
  320.5 87.4 %copy-start.8 = (s32[16,256]{1,0:T(8,128)S(1)}, s32[16,256]{1,0:T(8,128)}, u32[]{:S(2)}) copy-start(s32[16,256]{1,0:T(8,128)} %param.11) | copy-start | bytes 49156
  804.8 119.9 %copy-start = (f32[16,8,5,256]{3,2,1,0:T(8,128)}, f32[16,8,5,256]{3,2,1,0:T(8,128)S(1)}, u32[]{:S(2)}) copy-start(f32[16,8,5,256]{3,2,1,0:T(8,128)S(1)} %broadcast_maximum_fusion) | copy-start | bytes 1966084
  924.7 107.9 %copy-start.3 = (f32[16,8,5,256]{3,2,1,0:T(8,128)S(1)}, f32[16,8,5,256]{3,2,1,0:T(8,128)}, u32[]{:S(2)}) copy-start(f32[16,8,5,256]{3,2,1,0:T(8,128)} %get-tuple-element.384) | copy-start | bytes 1966084
  1033.0 94.9 %collective-permute-start = (bf16[16,256,8,128]{3,1,2,0:T(8,128)(2,1)}, bf16[16,256,8,128]{3,1,2,0:T(8,128)(2,1)}, u32[]{:S(2)}, u32[]{:S(2)}) collective-permute-start(bf16[16,256,8,128]{3,1,2,0:T(8,128)(2,1)} %get-tuple-element.393), channel_id=1, source_target_pairs={{0,1},{1,2},{2,3},{3,4},{4,5},{5,6},{6,7},{7,0}} | collective-permute-start | bytes 25165832 | tf_op jit(solution)/shard_map/while/body/eval_jaxpr/ppermute | solution.py:97
  1033.9 183.9 %collective-permute-start.1 = (bf16[16,256,8,128]{3,1,2,0:T(8,128)(2,1)}, bf16[16,256,8,128]{3,1,2,0:T(8,128)(2,1)}, u32[]{:S(2)}, u32[]{:S(2)}) collective-permute-start(bf16[16,256,8,128]{3,1,2,0:T(8,128)(2,1)} %get-tuple-element.394), channel_id=1, source_target_pairs={{0,1},{1,2},{2,3},{3,4},{4,5},{5,6},{6,7},{7,0}} | collective-permute-start | bytes 25165832 | tf_op jit(solution)/shard_map/while/body/eval_jaxpr/ppermute | solution.py:98
  1371.8 54.5 %copy-start.4 = (f32[16,8,5,128]{3,2,1,0:T(8,128)S(1)}, f32[16,8,5,128]{3,2,1,0:T(8,128)}, u32[]{:S(2)}) copy-start(f32[16,8,5,128]{3,2,1,0:T(8,128)} %get-tuple-element.293) | copy-start | bytes 983044 | tf_op jit(solution)/shard_map/while/body/eval_jaxpr/cond
  1371.8 54.5 %copy-start.5 = (f32[16,8,5,128]{3,2,1,0:T(8,128)S(1)}, f32[16,8,5,128]{3,2,1,0:T(8,128)}, u32[]{:S(2)}) copy-start(f32[16,8,5,128]{3,2,1,0:T(8,128)} %get-tuple-element.297) | copy-start | bytes 983044 | tf_op jit(solution)/shard_map/while/body/eval_jaxpr/cond
  1371.8 54.5 %copy-start.6 = (f32[16,8,5,128]{3,2,1,0:T(8,128)S(1)}, f32[16,8,5,128]{3,2,1,0:T(8,128)}, u32[]{:S(2)}) copy-start(f32[16,8,5,128]{3,2,1,0:T(8,128)} %get-tuple-element.298) | copy-start | bytes 983044 | tf_op jit(solution)/shard_map/while/body/eval_jaxpr/cond
  1445.5 93.8 %collective-permute-start = (bf16[16,256,8,128]{3,1,2,0:T(8,128)(2,1)}, bf16[16,256,8,128]{3,1,2,0:T(8,128)(2,1)}, u32[]{:S(2)}, u32[]{:S(2)}) collective-permute-start(bf16[16,256,8,128]{3,1,2,0:T(8,128)(2,1)} %get-tuple-element.393), channel_id=1, source_target_pairs={{0,1},{1,2},{2,3},{3,4},{4,5},{5,6},{6,7},{7,0}} | collective-permute-start | bytes 25165832 | tf_op jit(solution)/shard_map/while/body/eval_jaxpr/ppermute | solution.py:97
  1445.5 183.7 %collective-permute-start.1 = (bf16[16,256,8,128]{3,1,2,0:T(8,128)(2,1)}, bf16[16,256,8,128]{3,1,2,0:T(8,128)(2,1)}, u32[]{:S(2)}, u32[]{:S(2)}) collective-permute-start(bf16[16,256,8,128]{3,1,2,0:T(8,128)(2,1)} %get-tuple-element.394), channel_id=1, source_target_pairs={{0,1},{1,2},{2,3},{3,4},{4,5},{5,6},{6,7},{7,0}} | collective-permute-start | bytes 25165832 | tf_op jit(solution)/shard_map/while/body/eval_jaxpr/ppermute | solution.py:98
  1783.1 54.5 %copy-start.5 = (f32[16,8,5,128]{3,2,1,0:T(8,128)S(1)}, f32[16,8,5,128]{3,2,1,0:T(8,128)}, u32[]{:S(2)}) copy-start(f32[16,8,5,128]{3,2,1,0:T(8,128)} %get-tuple-element.297) | copy-start | bytes 983044 | tf_op jit(solution)/shard_map/while/body/eval_jaxpr/cond
  1783.2 54.5 %copy-start.6 = (f32[16,8,5,128]{3,2,1,0:T(8,128)S(1)}, f32[16,8,5,128]{3,2,1,0:T(8,128)}, u32[]{:S(2)}) copy-start(f32[16,8,5,128]{3,2,1,0:T(8,128)} %get-tuple-element.298) | copy-start | bytes 983044 | tf_op jit(solution)/shard_map/while/body/eval_jaxpr/cond
  1856.8 93.8 %collective-permute-start = (bf16[16,256,8,128]{3,1,2,0:T(8,128)(2,1)}, bf16[16,256,8,128]{3,1,2,0:T(8,128)(2,1)}, u32[]{:S(2)}, u32[]{:S(2)}) collective-permute-start(bf16[16,256,8,128]{3,1,2,0:T(8,128)(2,1)} %get-tuple-element.393), channel_id=1, source_target_pairs={{0,1},{1,2},{2,3},{3,4},{4,5},{5,6},{6,7},{7,0}} | collective-permute-start | bytes 25165832 | tf_op jit(solution)/shard_map/while/body/eval_jaxpr/ppermute | solution.py:97
  1856.8 183.7 %collective-permute-start.1 = (bf16[16,256,8,128]{3,1,2,0:T(8,128)(2,1)}, bf16[16,256,8,128]{3,1,2,0:T(8,128)(2,1)}, u32[]{:S(2)}, u32[]{:S(2)}) collective-permute-start(bf16[16,256,8,128]{3,1,2,0:T(8,128)(2,1)} %get-tuple-element.394), channel_id=1, source_target_pairs={{0,1},{1,2},{2,3},{3,4},{4,5},{5,6},{6,7},{7,0}} | collective-permute-start | bytes 25165832 | tf_op jit(solution)/shard_map/while/body/eval_jaxpr/ppermute | solution.py:98
  2194.5 54.5 %copy-start.5 = (f32[16,8,5,128]{3,2,1,0:T(8,128)S(1)}, f32[16,8,5,128]{3,2,1,0:T(8,128)}, u32[]{:S(2)}) copy-start(f32[16,8,5,128]{3,2,1,0:T(8,128)} %get-tuple-element.297) | copy-start | bytes 983044 | tf_op jit(solution)/shard_map/while/body/eval_jaxpr/cond
  2194.5 54.5 %copy-start.6 = (f32[16,8,5,128]{3,2,1,0:T(8,128)S(1)}, f32[16,8,5,128]{3,2,1,0:T(8,128)}, u32[]{:S(2)}) copy-start(f32[16,8,5,128]{3,2,1,0:T(8,128)} %get-tuple-element.298) | copy-start | bytes 983044 | tf_op jit(solution)/shard_map/while/body/eval_jaxpr/cond
  2268.1 93.8 %collective-permute-start = (bf16[16,256,8,128]{3,1,2,0:T(8,128)(2,1)}, bf16[16,256,8,128]{3,1,2,0:T(8,128)(2,1)}, u32[]{:S(2)}, u32[]{:S(2)}) collective-permute-start(bf16[16,256,8,128]{3,1,2,0:T(8,128)(2,1)} %get-tuple-element.393), channel_id=1, source_target_pairs={{0,1},{1,2},{2,3},{3,4},{4,5},{5,6},{6,7},{7,0}} | collective-permute-start | bytes 25165832 | tf_op jit(solution)/shard_map/while/body/eval_jaxpr/ppermute | solution.py:97
  2268.1 183.7 %collective-permute-start.1 = (bf16[16,256,8,128]{3,1,2,0:T(8,128)(2,1)}, bf16[16,256,8,128]{3,1,2,0:T(8,128)(2,1)}, u32[]{:S(2)}, u32[]{:S(2)}) collective-permute-start(bf16[16,256,8,128]{3,1,2,0:T(8,128)(2,1)} %get-tuple-element.394), channel_id=1, source_target_pairs={{0,1},{1,2},{2,3},{3,4},{4,5},{5,6},{6,7},{7,0}} | collective-permute-start | bytes 25165832 | tf_op jit(solution)/shard_map/while/body/eval_jaxpr/ppermute | solution.py:98
  2605.8 54.5 %copy-start.5 = (f32[16,8,5,128]{3,2,1,0:T(8,128)S(1)}, f32[16,8,5,128]{3,2,1,0:T(8,128)}, u32[]{:S(2)}) copy-start(f32[16,8,5,128]{3,2,1,0:T(8,128)} %get-tuple-element.297) | copy-start | bytes 983044 | tf_op jit(solution)/shard_map/while/body/eval_jaxpr/cond
  2605.8 54.5 %copy-start.6 = (f32[16,8,5,128]{3,2,1,0:T(8,128)S(1)}, f32[16,8,5,128]{3,2,1,0:T(8,128)}, u32[]{:S(2)}) copy-start(f32[16,8,5,128]{3,2,1,0:T(8,128)} %get-tuple-element.298) | copy-start | bytes 983044 | tf_op jit(solution)/shard_map/while/body/eval_jaxpr/cond
  2679.4 93.8 %collective-permute-start = (bf16[16,256,8,128]{3,1,2,0:T(8,128)(2,1)}, bf16[16,256,8,128]{3,1,2,0:T(8,128)(2,1)}, u32[]{:S(2)}, u32[]{:S(2)}) collective-permute-start(bf16[16,256,8,128]{3,1,2,0:T(8,128)(2,1)} %get-tuple-element.393), channel_id=1, source_target_pairs={{0,1},{1,2},{2,3},{3,4},{4,5},{5,6},{6,7},{7,0}} | collective-permute-start | bytes 25165832 | tf_op jit(solution)/shard_map/while/body/eval_jaxpr/ppermute | solution.py:97
  2679.4 183.7 %collective-permute-start.1 = (bf16[16,256,8,128]{3,1,2,0:T(8,128)(2,1)}, bf16[16,256,8,128]{3,1,2,0:T(8,128)(2,1)}, u32[]{:S(2)}, u32[]{:S(2)}) collective-permute-start(bf16[16,256,8,128]{3,1,2,0:T(8,128)(2,1)} %get-tuple-element.394), channel_id=1, source_target_pairs={{0,1},{1,2},{2,3},{3,4},{4,5},{5,6},{6,7},{7,0}} | collective-permute-start | bytes 25165832 | tf_op jit(solution)/shard_map/while/body/eval_jaxpr/ppermute | solution.py:98
  3017.1 54.5 %copy-start.5 = (f32[16,8,5,128]{3,2,1,0:T(8,128)S(1)}, f32[16,8,5,128]{3,2,1,0:T(8,128)}, u32[]{:S(2)}) copy-start(f32[16,8,5,128]{3,2,1,0:T(8,128)} %get-tuple-element.297) | copy-start | bytes 983044 | tf_op jit(solution)/shard_map/while/body/eval_jaxpr/cond
  3017.1 54.5 %copy-start.6 = (f32[16,8,5,128]{3,2,1,0:T(8,128)S(1)}, f32[16,8,5,128]{3,2,1,0:T(8,128)}, u32[]{:S(2)}) copy-start(f32[16,8,5,128]{3,2,1,0:T(8,128)} %get-tuple-element.298) | copy-start | bytes 983044 | tf_op jit(solution)/shard_map/while/body/eval_jaxpr/cond
  3090.7 93.8 %collective-permute-start = (bf16[16,256,8,128]{3,1,2,0:T(8,128)(2,1)}, bf16[16,256,8,128]{3,1,2,0:T(8,128)(2,1)}, u32[]{:S(2)}, u32[]{:S(2)}) collective-permute-start(bf16[16,256,8,128]{3,1,2,0:T(8,128)(2,1)} %get-tuple-element.393), channel_id=1, source_target_pairs={{0,1},{1,2},{2,3},{3,4},{4,5},{5,6},{6,7},{7,0}} | collective-permute-start | bytes 25165832 | tf_op jit(solution)/shard_map/while/body/eval_jaxpr/ppermute | solution.py:97
  3090.7 183.7 %collective-permute-start.1 = (bf16[16,256,8,128]{3,1,2,0:T(8,128)(2,1)}, bf16[16,256,8,128]{3,1,2,0:T(8,128)(2,1)}, u32[]{:S(2)}, u32[]{:S(2)}) collective-permute-start(bf16[16,256,8,128]{3,1,2,0:T(8,128)(2,1)} %get-tuple-element.394), channel_id=1, source_target_pairs={{0,1},{1,2},{2,3},{3,4},{4,5},{5,6},{6,7},{7,0}} | collective-permute-start | bytes 25165832 | tf_op jit(solution)/shard_map/while/body/eval_jaxpr/ppermute | solution.py:98
  3428.4 54.5 %copy-start.5 = (f32[16,8,5,128]{3,2,1,0:T(8,128)S(1)}, f32[16,8,5,128]{3,2,1,0:T(8,128)}, u32[]{:S(2)}) copy-start(f32[16,8,5,128]{3,2,1,0:T(8,128)} %get-tuple-element.297) | copy-start | bytes 983044 | tf_op jit(solution)/shard_map/while/body/eval_jaxpr/cond
  3428.4 54.5 %copy-start.6 = (f32[16,8,5,128]{3,2,1,0:T(8,128)S(1)}, f32[16,8,5,128]{3,2,1,0:T(8,128)}, u32[]{:S(2)}) copy-start(f32[16,8,5,128]{3,2,1,0:T(8,128)} %get-tuple-element.298) | copy-start | bytes 983044 | tf_op jit(solution)/shard_map/while/body/eval_jaxpr/cond
  3502.1 93.8 %collective-permute-start = (bf16[16,256,8,128]{3,1,2,0:T(8,128)(2,1)}, bf16[16,256,8,128]{3,1,2,0:T(8,128)(2,1)}, u32[]{:S(2)}, u32[]{:S(2)}) collective-permute-start(bf16[16,256,8,128]{3,1,2,0:T(8,128)(2,1)} %get-tuple-element.393), channel_id=1, source_target_pairs={{0,1},{1,2},{2,3},{3,4},{4,5},{5,6},{6,7},{7,0}} | collective-permute-start | bytes 25165832 | tf_op jit(solution)/shard_map/while/body/eval_jaxpr/ppermute | solution.py:97
  3502.1 183.7 %collective-permute-start.1 = (bf16[16,256,8,128]{3,1,2,0:T(8,128)(2,1)}, bf16[16,256,8,128]{3,1,2,0:T(8,128)(2,1)}, u32[]{:S(2)}, u32[]{:S(2)}) collective-permute-start(bf16[16,256,8,128]{3,1,2,0:T(8,128)(2,1)} %get-tuple-element.394), channel_id=1, source_target_pairs={{0,1},{1,2},{2,3},{3,4},{4,5},{5,6},{6,7},{7,0}} | collective-permute-start | bytes 25165832 | tf_op jit(solution)/shard_map/while/body/eval_jaxpr/ppermute | solution.py:98
  3839.7 54.5 %copy-start.5 = (f32[16,8,5,128]{3,2,1,0:T(8,128)S(1)}, f32[16,8,5,128]{3,2,1,0:T(8,128)}, u32[]{:S(2)}) copy-start(f32[16,8,5,128]{3,2,1,0:T(8,128)} %get-tuple-element.297) | copy-start | bytes 983044 | tf_op jit(solution)/shard_map/while/body/eval_jaxpr/cond
  3839.7 54.5 %copy-start.6 = (f32[16,8,5,128]{3,2,1,0:T(8,128)S(1)}, f32[16,8,5,128]{3,2,1,0:T(8,128)}, u32[]{:S(2)}) copy-start(f32[16,8,5,128]{3,2,1,0:T(8,128)} %get-tuple-element.298) | copy-start | bytes 983044 | tf_op jit(solution)/shard_map/while/body/eval_jaxpr/cond
  (15 other events, 638.9 us)
where the time goes:
time: 4180 us; the launch traced here: 4170 us
  matrix products  1430 us (34%)
  waiting for transfers between devices  1280 us (31%)
  other arithmetic  899 us (22%)
  local copies, waits for them, and re-layouts  553 us (13%)
    ppermute x7, waiting for transfers between devices, shift_step(): k_next = lax.ppermute(k_cur, 'cp', shift_pairs)  654 us
    ppermute x7, waiting for transfers between devices, shift_step(): v_next = lax.ppermute(v_cur, 'cp', shift_pairs)  629 us
    dot_general x8, matrix products, attend_block(): jnp.einsum('bhgqk,bkhd->bhgqd', exp_w.astype(jnp.bfloat16), v_blk, prefer...  502 us
    concatenate x7, other arithmetic, keys_after(): jnp.concatenate([acc_run[..., :half_len, :], acc_new], axis=-2)  381 us
    dot_general x8, matrix products, attend_block(): jnp.einsum('bqhgd,bkhd->bhgqk', q_rows, k_blk, preferred_element_type=jnp...  341 us
    dot_general x1, matrix products, output_proj(): jnp.einsum('bhgqd,hgde->bqe', normed, w_heads, preferred_element_type=jnp...  252 us
    reduce_sum x8, other arithmetic, attend_block(): l_new = rescale * l_run + jnp.sum(exp_w, axis=-1)  240 us
    dot_general x1, matrix products, project_qkv(): jnp.dot(flat_x, w_query, preferred_element_type=jnp.float32)  228 us
  transfers between devices with their start and end apart: 14, of which 14 were waited for; matrix products, arithmetic and copies ran while one was open for 0% of the time, Pallas kernels for 0%

commit v1 on v0

v1 whole, which is shorter than its diff:
```python
import functools
import math

import jax
import jax.numpy as jnp
from jax import lax
from jax.experimental import pallas as pl
from jax.experimental.pallas import tpu as pltpu
from jax.sharding import PartitionSpec as P

HEAD_DIM = 128
ROPE_BASE = 500000
MASK_FILL = -1e30
SCALE_LOG2 = HEAD_DIM ** -0.5 * math.log2(math.e)
GROUP = 5
KV_HEADS = 8
BLK = 128
PAIR = 2 * BLK
WIDTH = GROUP * BLK
N_ITEMS = 9
KV_COLS = KV_HEADS * HEAD_DIM
ROW_CHUNKS = (4, 6, 6)
MIB = 1024 * 1024


def rope_tables(positions):
    inv_freq = 1.0 / (ROPE_BASE ** (jnp.arange(0, HEAD_DIM, 2, dtype=jnp.float32) / HEAD_DIM))
    angles = positions.astype(jnp.float32)[:, :, None] * jnp.concatenate([inv_freq, inv_freq])
    sign = jnp.where(jnp.arange(HEAD_DIM) < HEAD_DIM // 2, -1.0, 1.0).astype(jnp.float32)
    return jnp.cos(angles), jnp.sin(angles) * sign


def rotate(vecs, cosv, sinv):
    return (vecs * cosv + pltpu.roll(vecs, HEAD_DIM // 2, 1) * sinv).astype(jnp.bfloat16)


def kv_kernel(chunks, x_ref, wk_ref, wv_ref, cos_ref, sin_ref, *out_refs):
    cosv, sinv = cos_ref[0], sin_ref[0]
    parts = []
    for c in range(0, KV_COLS, PAIR):
        acc = jnp.dot(x_ref[0], wk_ref[:, c:c + PAIR], preferred_element_type=jnp.float32)
        acc = acc.astype(jnp.bfloat16).astype(jnp.float32)
        parts.append((c, jnp.concatenate([rotate(acc[:, h:h + HEAD_DIM], cosv, sinv) for h in range(0, PAIR, HEAD_DIM)], axis=1)))
    for c in range(0, KV_COLS, PAIR):
        acc = jnp.dot(x_ref[0], wv_ref[:, c:c + PAIR], preferred_element_type=jnp.float32)
        parts.append((KV_COLS + c, acc.astype(jnp.bfloat16)))
    step = pl.program_id(0)
    first = 0
    for out_ref, rows in zip(out_refs, chunks):
        @pl.when((step >= first) & (step < first + rows))
        def _(out_ref=out_ref):
            for c, part in parts:
                out_ref[0, :, c:c + PAIR] = part
        first += rows


def project_kv(x, w_key, w_value, cos_t, sin_t, first_row, chunks):
    _, toks, dim = x.shape
    rows = sum(chunks)
    starts = [sum(chunks[:c]) for c in range(len(chunks))]

    def out_map(start, count):
        return lambda n: (jnp.clip(n - start, 0, count - 1), 0, 0)

    return pl.pallas_call(
        functools.partial(kv_kernel, chunks),
        grid=(rows,),
        out_shape=[jax.ShapeDtypeStruct((n, toks, 2 * KV_COLS), jnp.bfloat16) for n in chunks],
        in_specs=[
            pl.BlockSpec((1, toks, dim), lambda n: (n + first_row, 0, 0)),
            pl.BlockSpec((dim, KV_COLS), lambda n: (0, 0), pipeline_mode=pl.Buffered(1)),
            pl.BlockSpec((dim, KV_COLS), lambda n: (0, 0), pipeline_mode=pl.Buffered(1)),
            pl.BlockSpec((1, toks, HEAD_DIM), lambda n: (n + first_row, 0, 0)),
            pl.BlockSpec((1, toks, HEAD_DIM), lambda n: (n + first_row, 0, 0)),
        ],
        out_specs=[pl.BlockSpec((1, toks, 2 * KV_COLS), out_map(s, n)) for s, n in zip(starts, chunks)],
        compiler_params=pltpu.CompilerParams(dimension_semantics=('arbitrary',), vmem_limit_bytes=56 * MIB),
        cost_estimate=pl.CostEstimate(flops=2 * rows * toks * dim * 2 * KV_COLS, bytes_accessed=rows * toks * dim * 2 + dim * KV_COLS * 4, transcendentals=0),
        name='kv_proj',
    )(x, w_key, w_value, cos_t, sin_t)


def attn_kernel(n_steps, q_ref, cos_ref, sin_ref, k_ref, v_ref, o_ref, q_scr, s_scr, m_scr, mc_scr, l_scr, acc_scr):
    me = lax.axis_index('cp')
    step = pl.program_id(0)
    n_back = (17 - me) // 2
    n_front = (me + 2) // 2

    def block_at(ref, b):
        if isinstance(b, int):
            return ref[b, 0, :BLK, :] if b < 8 else ref[15 - b, 0, BLK:, :]
        late = (b >= 8).astype(jnp.int32)
        off = pl.multiple_of(late * BLK, BLK)
        return ref[b + late * (15 - 2 * b), 0, pl.ds(off, BLK), :]

    def pair_at(ref, p):
        return jnp.concatenate([block_at(ref, 2 * p), block_at(ref, 2 * p + 1)], axis=0)

    items = [(0, n_back - 1), (1, n_front - 1), (0, 0), (0, 1), (0, 2), (0, 3)]
    for u in range(3):
        front = (u < n_front - 1).astype(jnp.int32)
        items.append((front, u + (1 - front) * (5 - n_front)))

    def finish(col):
        for half in range(2):
            rows = slice(BLK, 2 * BLK) if half == 0 else slice(0, BLK)
            inv = 1.0 / jnp.sum(l_scr[half], axis=0, keepdims=True)
            out_t = (acc_scr[half] * inv).astype(jnp.bfloat16)
            for g in range(GROUP):
                o_ref[0, rows, pl.ds(pl.multiple_of(col + g * HEAD_DIM, HEAD_DIM), HEAD_DIM)] = out_t[:, g * BLK:(g + 1) * BLK].T

    finish((step % 2) * WIDTH)

    for half in range(2):
        rows = slice(BLK, 2 * BLK) if half == 0 else slice(0, BLK)
        cosv, sinv = cos_ref[0, rows, :], sin_ref[0, rows, :]
        for g in range(GROUP):
            q_scr[half, g * BLK:(g + 1) * BLK, :] = rotate(q_ref[0, rows, g * HEAD_DIM:(g + 1) * HEAD_DIM].astype(jnp.float32), cosv, sinv)

    def weights(t):
        half, pair = items[t]
        e = jnp.exp2(s_scr[t] * SCALE_LOG2 - mc_scr[half])
        part = jnp.sum(e.reshape(PAIR // 8, 8, WIDTH), axis=0)
        return part, jnp.dot(pair_at(v_ref, pair).T, e.astype(jnp.bfloat16), preferred_element_type=jnp.float32)

    def new_scores(t):
        half, pair = items[t]
        s_new = lax.dot_general(pair_at(k_ref, pair), q_scr[half], (((1,), (1,)), ((), ())), preferred_element_type=jnp.float32)
        if t < 2:
            q_blk = 15 - me if t == 0 else me
            key_tok = lax.broadcasted_iota(jnp.int32, (PAIR, BLK), 0) + pair * PAIR
            q_tok = lax.broadcasted_iota(jnp.int32, (PAIR, BLK), 1) + q_blk * BLK
            keep = jnp.concatenate([key_tok <= q_tok] * GROUP, axis=1)
            s_new = jnp.where(keep, s_new, MASK_FILL)
        s_scr[t] = s_new
        return jnp.max(s_new.reshape(PAIR // 8, 8, WIDTH), axis=0)

    l_sum, acc, top = [None, None], [None, None], [None, None]
    for t in range(6):
        half = items[t][0]
        part, pv = weights(t)
        l_sum[half] = part if l_sum[half] is None else l_sum[half] + part
        acc[half] = pv if acc[half] is None else acc[half] + pv
        peak = new_scores(t)
        top[half] = peak if top[half] is None else jnp.maximum(top[half], peak)
    for half in range(2):
        l_scr[half], acc_scr[half], m_scr[half] = l_sum[half], acc[half], top[half]
    for t in range(6, N_ITEMS):
        half = items[t][0]
        part, pv = weights(t)
        l_scr[half] += part
        acc_scr[half] += pv
        m_scr[half] = jnp.maximum(m_scr[half], new_scores(t))
    for half in range(2):
        mc_scr[half] = jnp.max(m_scr[half], axis=0, keepdims=True) * SCALE_LOG2

    @pl.when(step == n_steps)
    def _():
        finish(WIDTH)


def attention(q, cos_t, sin_t, kv_all, first_row):
    rows = kv_all.shape[1]
    toks = q.shape[1]
    n_steps = rows * KV_HEADS

    def cur(n):
        m = jnp.minimum(n, n_steps - 1)
        return m // KV_HEADS, m % KV_HEADS

    def prev(n, back=1):
        m = jnp.maximum(n - back, 0)
        return m // KV_HEADS, m % KV_HEADS

    flops = n_steps * N_ITEMS * 4 * PAIR * WIDTH * HEAD_DIM
    return pl.pallas_call(
        functools.partial(attn_kernel, n_steps),
        grid=(n_steps + 1,),
        out_shape=jax.ShapeDtypeStruct((rows,) + q.shape[1:], jnp.bfloat16),
        in_specs=[
            pl.BlockSpec((1, toks, WIDTH), lambda n: (cur(n)[0] + first_row, 0, cur(n)[1])),
            pl.BlockSpec((1, toks, HEAD_DIM), lambda n: (cur(n)[0] + first_row, 0, 0)),
            pl.BlockSpec((1, toks, HEAD_DIM), lambda n: (cur(n)[0] + first_row, 0, 0)),
            pl.BlockSpec((8, 1, toks, HEAD_DIM), lambda n: (0, cur(n)[0], 0, cur(n)[1])),
            pl.BlockSpec((8, 1, toks, HEAD_DIM), lambda n: (0, prev(n)[0], 0, KV_HEADS + prev(n)[1])),
        ],
        out_specs=pl.BlockSpec((1, toks, 2 * WIDTH), lambda n: (prev(n, 2)[0], 0, prev(n, 2)[1] // 2)),
        scratch_shapes=[
            pltpu.VMEM((2, WIDTH, HEAD_DIM), jnp.bfloat16),
            pltpu.VMEM((N_ITEMS, PAIR, WIDTH), jnp.float32),
            pltpu.VMEM((2, 8, WIDTH), jnp.float32),
            pltpu.VMEM((2, 1, WIDTH), jnp.float32),
            pltpu.VMEM((2, 8, WIDTH), jnp.float32),
            pltpu.VMEM((2, HEAD_DIM, WIDTH), jnp.float32),
        ],
        compiler_params=pltpu.CompilerParams(dimension_semantics=('arbitrary',), vmem_limit_bytes=40 * MIB),
        cost_estimate=pl.CostEstimate(flops=flops, bytes_accessed=rows * toks * (16 * 2 * KV_COLS + 4 * 5120), transcendentals=flops // (4 * HEAD_DIM)),
        name='attn',
    )(q, cos_t, sin_t, kv_all, kv_all)


def unset(shape):
    return pl.pallas_call(
        lambda out_ref: None,
        out_shape=jax.ShapeDtypeStruct(shape, jnp.bfloat16),
        out_specs=pl.BlockSpec(memory_space=pl.ANY),
        name='unset',
    )()


def solution(mesh):
    row_spec = P('data', 'cp', None)
    rep_spec = P(None, None)

    def local_block(x, pos, w_query, w_key, w_value, w_out):
        cos_t, sin_t = rope_tables(pos)
        kv = project_kv(x, w_key, w_value, cos_t, sin_t, 0, ROW_CHUNKS[:1])
        x, kv = lax.optimization_barrier((x, kv))
        kv += project_kv(x, w_key, w_value, cos_t, sin_t, ROW_CHUNKS[0], ROW_CHUNKS[1:])
        gathered = [lax.all_gather(part, 'cp') for part in kv]
        x, kv = lax.optimization_barrier((x, kv))
        q = jnp.einsum('bte,ed->btd', x, w_query, preferred_element_type=jnp.float32).astype(jnp.bfloat16)
        y = unset(x.shape)
        first = 0
        for kv_all in gathered:
            span = slice(first, first + kv_all.shape[1])
            o = attention(q, cos_t, sin_t, kv_all, first)
            part = jnp.einsum('btd,de->bte', o, w_out, preferred_element_type=jnp.float32)
            y = y.at[span].set((x[span].astype(jnp.float32) + part).astype(jnp.bfloat16))
            q, y = lax.optimization_barrier((q, y))
            first = span.stop
        return y

    return jax.shard_map(local_block, mesh=mesh, in_specs=(row_spec, P('data', 'cp'), rep_spec, rep_spec, rep_spec, rep_spec), out_specs=row_spec, check_vma=False)
```

time: 4180 us -> 898 us (0.21)
  waiting for transfers between devices: 1280 us -> 0.55 us
  matrix products: 1430 us -> 477 us
  other arithmetic: 899 us -> 9.7 us
  local copies, waits for them, and re-layouts: 553 us -> 4.77 us
  Pallas kernels: 0 us -> 385 us
    ppermute x14 -> x0, waiting for transfers between devices: 1280 us -> none  [the longest x7 654 us: shift_step(): k_next = lax.ppermute(k_cur, 'cp', shift_pairs)]
    dot_general x20 -> x4, matrix products: 1430 us -> 477 us  [the longest x3 249 us: local_block(): jnp.einsum('btd,de->bte', o, w_out, preferred_element_type=jnp.float32)]
    concatenate x16 -> x0, other arithmetic: 437 us -> none  [the longest x7 381 us: keys_after(): jnp.concatenate([acc_run[..., :half_len, :], acc_new], axis=-2)]
    pallas_call x0 -> x6, Pallas kernels: none -> 385 us  [the longest x3 274 us: attention(): pl.pallas_call(functools.partial(attn_kernel, n_steps), grid=(n_steps + 1...]
    slice x9 -> x0, local copies, waits for them, and re-layouts: 301 us -> none  [the longest x7 202 us: keys_after(): acc_run[..., :half_len, :]]
    reduce_sum x8 -> x0, other arithmetic: 240 us -> none  [attend_block(): l_new = rescale * l_run + jnp.sum(exp_w, axis=-1)]
    another operation x3 -> x0, other arithmetic: 194 us -> none
    while x22 -> x0, local copies, waits for them, and re-layouts: 135 us -> none
  transfers between devices with their start and end apart: 14 -> 3, of which waited for: 14 -> 0; matrix products, arithmetic and copies ran while one was open for 0% -> 43% of each run, Pallas kernels for 0% -> 28%
where the time goes in v1:
time: 898 us; the launch traced here: 891 us
  matrix products  477 us (53%)
  Pallas kernels  385 us (43%)
  between operations  13.6 us (2%)
  other arithmetic  9.7 us (1%)
    pallas_call x3, Pallas kernels, attention(): pl.pallas_call(functools.partial(attn_kernel, n_steps), grid=(n_steps + 1...  274 us
    dot_general x3, matrix products, local_block(): jnp.einsum('btd,de->bte', o, w_out, preferred_element_type=jnp.float32)  249 us
    dot_general x1, matrix products, local_block(): jnp.einsum('bte,ed->btd', x, w_query, preferred_element_type=jnp.float32)  228 us
    pallas_call x2, Pallas kernels, project_kv(): pl.pallas_call(functools.partial(kv_kernel, chunks), grid=(rows,), out_sh...  111 us
  transfers between devices with their start and end apart: 3, of which 0 were waited for; matrix products, arithmetic and copies ran while one was open for 43% of the time, Pallas kernels for 28%

profile of v1, /device:TPU:0, one launch (start us, length us, event | category | flops | bytes accessed | tf_op | source)
XLA Modules:
  0.0 891.1 jit_solution(7529170796944934822)
XLA Ops:
  6.5 0.0 all-gather.7.cloned.1.call-start
  6.5 0.1 compare_select_fusion
  6.6 0.7 convert_element_type.24
  7.4 8.9 fusion.22
  16.2 32.0 %kv_proj.2 = bf16[4,256,2048]{2,1,0:T(8,128)(2,1)} custom-call(bf16[16,256,5120]{2,1,0:T(8,128)(2,1)} %x_ref.2, bf16[5120,1024]{1,0:T(8,128)(2,1)} %wk_ref.3, bf16[5120,1024]{1,0:T(8,128)(2,1)} %wv_ref.3, f32[16,256,128]{2,1,0:T(8,128)} %get-tuple-element.62.cos_ref, f32[16,256,128]{2,1,0:T(8,128)} %get-tuple-element.61.sin_ref), custom_call_target="tpu_custom_call" | custom-call | flops 21474836480 | bytes 31457280 | tf_op jit(solution)/shard_map/kv_proj/pallas_call | solution.py:65
  48.3 0.0 all-gather.7.cloned.1.call-update
  48.3 0.0 all-gather.9.cloned.1.call-start
  48.3 79.2 %kv_proj.3 = (bf16[6,256,2048]{2,1,0:T(8,128)(2,1)}, bf16[6,256,2048]{2,1,0:T(8,128)(2,1)}) custom-call(bf16[16,256,5120]{2,1,0:T(8,128)(2,1)} %x_ref.2, bf16[5120,1024]{1,0:T(8,128)(2,1)} %wk_ref.3, bf16[5120,1024]{1,0:T(8,128)(2,1)} %wv_ref.3, f32[16,256,128]{2,1,0:T(8,128)} %get-tuple-element.62.cos_ref, f32[16,256,128]{2,1,0:T(8,128)} %get-tuple-element.61.sin_ref), custom_call_target="tpu_custom_call" | custom-call | flops 64424509440 | bytes 52428800 | tf_op jit(solution)/shard_map/kv_proj/pallas_call | solution.py:65
  127.5 0.0 all-gather.9.cloned.1.call-update
  127.5 0.2 all-gather.11.cloned.1.call-start
  127.8 0.5 all-gather.11.cloned.1.call-update
  128.3 0.0 copy-start
  128.3 228.2 %fusion.8.q_ref = bf16[16,256,5120]{2,1,0:T(8,128)(2,1)} fusion(bf16[16,256,5120]{2,1,0:T(8,128)(2,1)} %x_ref.2, bf16[5120,5120]{1,0:T(8,128)(2,1)} %param.14), kind=kOutput, calls=%fused_computation.8 | convolution fusion | flops 214769336320 | bytes 136314880 | tf_op jit(solution)/shard_map/bte,ed->btd/dot_general | solution.py:222
  356.5 0.0 all-gather.7.cloned.1.call-done
  356.5 0.0 copy-done
  356.5 0.0 copy-start.1
  356.5 1.6 copy-done.1
  358.1 68.9 %attn.3 = bf16[4,256,5120]{2,1,0:T(8,128)(2,1)} custom-call(bf16[16,256,5120]{2,1,0:T(8,128)(2,1)} %fusion.8.q_ref, f32[16,256,128]{2,1,0:T(8,128)S(1)} %copy-done.1, f32[16,256,128]{2,1,0:T(8,128)S(1)} %copy-done, bf16[8,4,256,2048]{3,2,1,0:T(8,128)(2,1)} %bitcast.31, bf16[8,4,256,2048]{3,2,1,0:T(8,128)(2,1)} %bitcast.32), custom_call_target="tpu_custom_call" | custom-call | flops 24159191040 | bytes 54525952 | tf_op jit(solution)/shard_map/attn/pallas_call | solution.py:176
  427.0 64.1 %fusion.19 = bf16[16,256,5120]{2,1,0:T(8,128)(2,1)} fusion(bf16[16,256,5120]{2,1,0:T(8,128)(2,1)} %unset.1, bf16[4,256,5120]{2,1,0:T(8,128)(2,1)} %attn.3, bf16[5120,5120]{1,0:T(8,128)(2,1)} %param.17, bf16[16,256,5120]{2,1,0:T(8,128)(2,1)} %x_ref.2), kind=kOutput, calls=%fused_computation.14 | convolution fusion | flops 53702819840 | bytes 83886080 | tf_op jit(solution)/shard_map/btd,de->bte/dot_general | solution.py:228
  491.2 0.0 all-gather.9.cloned.1.call-done
  491.2 0.0 copy-start.2
  491.2 1.6 copy-done.2
  492.8 102.3 %attn.4 = bf16[6,256,5120]{2,1,0:T(8,128)(2,1)} custom-call(bf16[16,256,5120]{2,1,0:T(8,128)(2,1)} %fusion.8.q_ref, f32[16,256,128]{2,1,0:T(8,128)S(1)} %copy-done.2, f32[16,256,128]{2,1,0:T(8,128)S(1)} %copy-done, bf16[8,6,256,2048]{3,2,1,0:T(8,128)(2,1)} %bitcast.27, bf16[8,6,256,2048]{3,2,1,0:T(8,128)(2,1)} %bitcast.28), custom_call_target="tpu_custom_call" | custom-call | flops 36238786560 | bytes 81788928 | tf_op jit(solution)/shard_map/attn/pallas_call | solution.py:176
  595.1 92.5 %fusion.11 = bf16[16,256,5120]{2,1,0:T(8,128)(2,1)} fusion(bf16[16,256,5120]{2,1,0:T(8,128)(2,1)} %fusion.19, bf16[16,256,5120]{2,1,0:T(8,128)(2,1)} %x_ref.2, bf16[6,256,5120]{2,1,0:T(8,128)(2,1)} %attn.4, bf16[5120,5120]{1,0:T(8,128)(2,1)} %param.17), kind=kOutput, calls=%fused_computation.12 | convolution fusion | flops 80554229760 | bytes 99614720 | tf_op jit(solution)/shard_map/btd,de->bte/dot_general | solution.py:228
  687.6 0.0 all-gather.11.cloned.1.call-done
  687.6 0.0 copy-start.3
  687.6 1.6 copy-done.3
  689.2 102.3 %attn.5 = bf16[6,256,5120]{2,1,0:T(8,128)(2,1)} custom-call(bf16[16,256,5120]{2,1,0:T(8,128)(2,1)} %fusion.8.q_ref, f32[16,256,128]{2,1,0:T(8,128)S(1)} %copy-done.3, f32[16,256,128]{2,1,0:T(8,128)S(1)} %copy-done, bf16[8,6,256,2048]{3,2,1,0:T(8,128)(2,1)} %bitcast.29, bf16[8,6,256,2048]{3,2,1,0:T(8,128)(2,1)} %bitcast.30), custom_call_target="tpu_custom_call" | custom-call | flops 36238786560 | bytes 81788928 | tf_op jit(solution)/shard_map/attn/pallas_call | solution.py:176
  791.6 92.6 %fusion.12 = bf16[16,256,5120]{2,1,0:T(8,128)(2,1)} fusion(bf16[16,256,5120]{2,1,0:T(8,128)(2,1)} %fusion.11, bf16[16,256,5120]{2,1,0:T(8,128)(2,1)} %x_ref.2, bf16[6,256,5120]{2,1,0:T(8,128)(2,1)} %attn.5, bf16[5120,5120]{1,0:T(8,128)(2,1)} %param.17), kind=kOutput, calls=%fused_computation.13 | convolution fusion | flops 80554229760 | bytes 99614720 | tf_op jit(solution)/shard_map/btd,de->bte/dot_general | solution.py:228
  (2 shorter events, 0.0 us)
Async XLA Ops:
  6.5 350.0 %all-gather.7.cloned.1.call-start = ((), (), s32[]{:S(2)}) async-start(), calls=%async_computation | async-start | bytes 37748736 | tf_op jit(solution)/shard_map/all_gather | solution.py:220
  48.3 442.9 %all-gather.9.cloned.1.call-start = ((), (), s32[]{:S(2)}) async-start(), calls=%async_computation.1 | async-start | bytes 56623104 | tf_op jit(solution)/shard_map/all_gather | solution.py:220
  127.5 560.1 %all-gather.11.cloned.1.call-start = ((), (), s32[]{:S(2)}) async-start(), calls=%async_computation.2 | async-start | bytes 56623104 | tf_op jit(solution)/shard_map/all_gather | solution.py:220
  128.3 228.2 %copy-start = (f32[16,256,128]{2,1,0:T(8,128)S(1)}, f32[16,256,128]{2,1,0:T(8,128)}, u32[]{:S(2)}) copy-start(f32[16,256,128]{2,1,0:T(8,128)} %get-tuple-element.61.sin_ref) | copy-start | bytes 6291460
  356.5 1.6 copy-start.1
  491.2 1.6 copy-start.2
  687.6 1.6 copy-start.3
Sparse Core Ops, SparseCore 0:
  48.4 158.0 all-gather.6
  208.3 226.6 all-gather.8
  436.8 226.5 all-gather.10

commit v2 on v1

v2 whole, which is shorter than its diff:
```python
import functools
import math

import jax
import jax.numpy as jnp
from jax import lax
from jax.experimental import pallas as pl
from jax.experimental.pallas import tpu as pltpu
from jax.sharding import PartitionSpec as P

HEAD_DIM = 128
ROPE_BASE = 500000
MASK_FILL = -1e30
SCALE_LOG2 = HEAD_DIM ** -0.5 * math.log2(math.e)
GROUP = 5
KV_HEADS = 8
BLK = 128
PAIR = 2 * BLK
WIDTH = GROUP * BLK
N_BLOCKS = 17
ROWS = 2
KV_COLS = KV_HEADS * HEAD_DIM
ROW_CHUNKS = (6, 6, 4)
MIB = 1024 * 1024


def rope_tables(positions):
    inv_freq = 1.0 / (ROPE_BASE ** (jnp.arange(0, HEAD_DIM, 2, dtype=jnp.float32) / HEAD_DIM))
    angles = positions.astype(jnp.float32)[:, :, None] * jnp.concatenate([inv_freq, inv_freq])
    sign = jnp.where(jnp.arange(HEAD_DIM) < HEAD_DIM // 2, -1.0, 1.0).astype(jnp.float32)
    return jnp.cos(angles), jnp.sin(angles) * sign


def rotate(vecs, cosv, sinv):
    return (vecs * cosv + pltpu.roll(vecs, HEAD_DIM // 2, 1) * sinv).astype(jnp.bfloat16)


def turn_into(out_ref, raw_ref, cos_ref, sin_ref, c):
    for h in range(c, c + PAIR, HEAD_DIM):
        vecs = raw_ref[:, h:h + HEAD_DIM].astype(jnp.float32)
        out_ref[:, :, h:h + HEAD_DIM] = rotate(vecs, flat(cos_ref), flat(sin_ref)).reshape(out_ref.shape[:2] + (HEAD_DIM,))


def flat(ref):
    rows, toks, cols = ref.shape
    return ref[...].reshape(rows * toks, cols)


def kv_kernel(chunks, x_ref, wk_ref, wv_ref, cos_ref, sin_ref, *refs):
    out_refs, (raw_scr,) = refs[:len(chunks)], refs[len(chunks):]
    step = pl.program_id(0)
    first = 0
    for out_ref, count in zip(out_refs, chunks):
        @pl.when((step >= first) & (step < first + count // ROWS))
        def _(out_ref=out_ref):
            for c in range(0, KV_COLS, PAIR):
                raw_scr[:, c:c + PAIR] = jnp.dot(flat(x_ref), wk_ref[:, c:c + PAIR], preferred_element_type=jnp.float32).astype(jnp.bfloat16)
            for c in range(0, KV_COLS, PAIR):
                turn_into(out_ref, raw_scr, cos_ref, sin_ref, c)
                acc = jnp.dot(flat(x_ref), wv_ref[:, c:c + PAIR], preferred_element_type=jnp.float32).astype(jnp.bfloat16)
                out_ref[:, :, KV_COLS + c:KV_COLS + c + PAIR] = acc.reshape(out_ref.shape[:2] + (PAIR,))
        first += count // ROWS


def project_kv(x, w_key, w_value, cos_t, sin_t, first_row, chunks):
    _, toks, dim = x.shape
    total = sum(chunks)
    starts = [sum(chunks[:c]) for c in range(len(chunks))]

    def block(cols):
        return pl.BlockSpec((ROWS, toks, cols), lambda n: (n + first_row // ROWS, 0, 0))

    weights = pl.BlockSpec((dim, KV_COLS), lambda n: (0, 0), pipeline_mode=pl.Buffered(1))

    def out_map(start, count):
        return lambda n: (jnp.clip(n - start // ROWS, 0, count // ROWS - 1), 0, 0)

    return pl.pallas_call(
        functools.partial(kv_kernel, chunks),
        grid=(total // ROWS,),
        out_shape=[jax.ShapeDtypeStruct((n, toks, 2 * KV_COLS), jnp.bfloat16) for n in chunks],
        in_specs=[block(dim), weights, weights, block(HEAD_DIM), block(HEAD_DIM)],
        out_specs=[pl.BlockSpec((ROWS, toks, 2 * KV_COLS), out_map(s, n)) for s, n in zip(starts, chunks)],
        scratch_shapes=[pltpu.VMEM((ROWS * toks, KV_COLS), jnp.bfloat16)],
        compiler_params=pltpu.CompilerParams(dimension_semantics=('arbitrary',), vmem_limit_bytes=56 * MIB),
        cost_estimate=pl.CostEstimate(flops=2 * total * toks * dim * 2 * KV_COLS, bytes_accessed=total * toks * dim * 2 + dim * KV_COLS * 4, transcendentals=0),
        name='kv_proj',
    )(x, w_key, w_value, cos_t, sin_t)


def q_kernel(n_tiles, x_ref, w_ref, cos_ref, sin_ref, q_ref, raw_scr):
    step = pl.program_id(0)

    @pl.when(step < n_tiles)
    def _():
        for c in range(0, q_ref.shape[2], PAIR):
            turn_into(q_ref, raw_scr, cos_ref, sin_ref, c)
            raw_scr[:, c:c + PAIR] = jnp.dot(flat(x_ref), w_ref[:, c:c + PAIR], preferred_element_type=jnp.float32).astype(jnp.bfloat16)

    @pl.when(step == n_tiles)
    def _():
        for c in range(0, q_ref.shape[2], PAIR):
            turn_into(q_ref, raw_scr, cos_ref, sin_ref, c)


def project_q(x, w_query, cos_t, sin_t):
    rows, toks, dim = x.shape
    cols, group = 512, 2 * ROWS
    across = w_query.shape[1] // cols
    n_tiles = rows // group * across

    def cur(n):
        m = jnp.minimum(n, n_tiles - 1)
        return m // across, m % across

    def prev(n):
        m = jnp.maximum(n - 1, 0)
        return m // across, m % across

    table = pl.BlockSpec((group, toks, HEAD_DIM), lambda n: (prev(n)[0], 0, 0))
    return pl.pallas_call(
        functools.partial(q_kernel, n_tiles),
        grid=(n_tiles + 1,),
        out_shape=jax.ShapeDtypeStruct((rows, toks, w_query.shape[1]), jnp.bfloat16),
        in_specs=[
            pl.BlockSpec((group, toks, dim), lambda n: (cur(n)[0], 0, 0)),
            pl.BlockSpec((dim, cols), lambda n: (0, cur(n)[1])),
            table, table,
        ],
        out_specs=pl.BlockSpec((group, toks, cols), lambda n: (prev(n)[0], 0, prev(n)[1])),
        scratch_shapes=[pltpu.VMEM((group * toks, cols), jnp.bfloat16)],
        compiler_params=pltpu.CompilerParams(dimension_semantics=('arbitrary',), vmem_limit_bytes=56 * MIB),
        cost_estimate=pl.CostEstimate(flops=2 * rows * toks * dim * w_query.shape[1], bytes_accessed=2 * x.size * 2 + w_query.size * 2, transcendentals=0),
        name='q_proj',
    )(x, w_query, cos_t, sin_t)


def attn_kernel(n_steps, q_ref, k_ref, v_ref, o_ref, s_scr, m_scr, mc_scr, l_scr, acc_scr, l_done, acc_done):
    me = lax.axis_index('cp')
    step = pl.program_id(0)

    def block_at(ref, b):
        if isinstance(b, int):
            return ref[b, 0, :BLK, :] if b < 8 else ref[15 - b, 0, BLK:, :]
        late = (b >= 8).astype(jnp.int32)
        off = pl.multiple_of(late * BLK, BLK)
        return ref[b + late * (15 - 2 * b), 0, pl.ds(off, BLK), :]

    def keys_at(ref, blocks):
        return jnp.concatenate([block_at(ref, b) for b in blocks], axis=0)

    odd = me % 2
    items = [(0, (15 - me, 0, 1)), (1, (me,)), (odd, (14 - me + odd * (2 * me - 15),)), (0, (2, 3)), (0, (4, 5)), (0, (6, 7))]
    for u in range(3):
        front = (u < me // 2).astype(jnp.int32)
        pair = u + (1 - front) * (4 - me // 2)
        items.append((front, (2 * pair, 2 * pair + 1)))
    ends = [0]
    for _, blocks in items:
        ends.append(ends[-1] + BLK * len(blocks))

    def half_rows(half):
        return slice(BLK, 2 * BLK) if half == 0 else slice(0, BLK)

    def queries(half):
        off = (1 - half) * BLK
        off = off if isinstance(off, int) else pl.multiple_of(off, BLK)
        return jnp.concatenate([q_ref[0, pl.ds(off, BLK), g * HEAD_DIM:(g + 1) * HEAD_DIM] for g in range(GROUP)], axis=0)

    def finish(l_in, acc_in, col):
        for half in range(2):
            inv = 1.0 / jnp.sum(l_in[half], axis=0, keepdims=True)
            out_t = (acc_in[half] * inv).astype(jnp.bfloat16)
            for g in range(GROUP):
                o_ref[0, half_rows(half), pl.ds(pl.multiple_of(col + g * HEAD_DIM, HEAD_DIM), HEAD_DIM)] = out_t[:, g * BLK:(g + 1) * BLK].T

    l_done[...] = l_scr[...]
    acc_done[...] = acc_scr[...]
    for t, (half, blocks) in enumerate(items):
        n_keys = ends[t + 1] - ends[t]
        span = slice(ends[t], ends[t + 1])
        vt = keys_at(v_ref, blocks).T
        e = jnp.exp2(s_scr[span] * SCALE_LOG2 - mc_scr[half])
        part = jnp.sum(e.reshape(n_keys // 8, 8, WIDTH), axis=0)
        pv = jnp.dot(vt, e.astype(jnp.bfloat16), preferred_element_type=jnp.float32)
        if t < 2:
            l_scr[half], acc_scr[half] = part, pv
        else:
            l_scr[half] += part
            acc_scr[half] += pv
        s_new = lax.dot_general(keys_at(k_ref, blocks), queries(half), (((1,), (1,)), ((), ())), preferred_element_type=jnp.float32)
        if t < 2:
            keep = lax.broadcasted_iota(jnp.int32, (BLK, BLK), 0) <= lax.broadcasted_iota(jnp.int32, (BLK, BLK), 1)
            masked = jnp.where(jnp.concatenate([keep] * GROUP, axis=1), s_new[:BLK], MASK_FILL)
            s_new = jnp.concatenate([masked, s_new[BLK:]], axis=0) if n_keys > BLK else masked
        s_scr[span] = s_new
        peak = jnp.max(s_new.reshape(n_keys // 8, 8, WIDTH), axis=0)
        m_scr[half] = peak if t < 2 else jnp.maximum(m_scr[half], peak)
        if t == 8:
            finish(l_done, acc_done, (step % 2) * WIDTH)
    for half in range(2):
        mc_scr[half] = jnp.max(m_scr[half], axis=0, keepdims=True) * SCALE_LOG2

    @pl.when(step == n_steps)
    def _():
        finish(l_scr, acc_scr, WIDTH)


def attention(q, kv_all, first_row):
    rows = kv_all.shape[1]
    toks = q.shape[1]
    n_steps = rows * KV_HEADS

    def head_of(n):
        m = jnp.clip(n, 0, n_steps - 1)
        return m // KV_HEADS, m % KV_HEADS

    flops = n_steps * N_BLOCKS * 4 * BLK * WIDTH * HEAD_DIM
    return pl.pallas_call(
        functools.partial(attn_kernel, n_steps),
        grid=(n_steps + 1,),
        out_shape=jax.ShapeDtypeStruct((rows,) + q.shape[1:], jnp.bfloat16),
        in_specs=[
            pl.BlockSpec((1, toks, WIDTH), lambda n: (head_of(n)[0] + first_row, 0, head_of(n)[1])),
            pl.BlockSpec((8, 1, toks, HEAD_DIM), lambda n: (0, head_of(n)[0], 0, head_of(n)[1])),
            pl.BlockSpec((8, 1, toks, HEAD_DIM), lambda n: (0, head_of(n - 1)[0], 0, KV_HEADS + head_of(n - 1)[1])),
        ],
        out_specs=pl.BlockSpec((1, toks, 2 * WIDTH), lambda n: (head_of(n - 2)[0], 0, head_of(n - 2)[1] // 2)),
        scratch_shapes=[
            pltpu.VMEM((N_BLOCKS * BLK, WIDTH), jnp.float32),
            pltpu.VMEM((2, 8, WIDTH), jnp.float32),
            pltpu.VMEM((2, 1, WIDTH), jnp.float32),
            pltpu.VMEM((2, 8, WIDTH), jnp.float32),
            pltpu.VMEM((2, HEAD_DIM, WIDTH), jnp.float32),
            pltpu.VMEM((2, 8, WIDTH), jnp.float32),
            pltpu.VMEM((2, HEAD_DIM, WIDTH), jnp.float32),
        ],
        compiler_params=pltpu.CompilerParams(dimension_semantics=('arbitrary',), vmem_limit_bytes=58 * MIB),
        cost_estimate=pl.CostEstimate(flops=flops, bytes_accessed=rows * toks * (16 * 2 * KV_COLS + 4 * 5120), transcendentals=flops // (4 * HEAD_DIM)),
        name='attn',
    )(q, kv_all, kv_all)


def unset(shape):
    return pl.pallas_call(
        lambda out_ref: None,
        out_shape=jax.ShapeDtypeStruct(shape, jnp.bfloat16),
        out_specs=pl.BlockSpec(memory_space=pl.ANY),
        name='unset',
    )()


def solution(mesh):
    row_spec = P('data', 'cp', None)
    rep_spec = P(None, None)

    def local_block(x, pos, w_query, w_key, w_value, w_out):
        cos_t, sin_t = rope_tables(pos)
        kv = project_kv(x, w_key, w_value, cos_t, sin_t, 0, ROW_CHUNKS[:1])
        x, kv = lax.optimization_barrier((x, kv))
        kv += project_kv(x, w_key, w_value, cos_t, sin_t, ROW_CHUNKS[0], ROW_CHUNKS[1:])
        gathered = [lax.all_gather(part, 'cp') for part in kv]
        x, kv = lax.optimization_barrier((x, kv))
        q = project_q(x, w_query, cos_t, sin_t)
        y, first = unset(x.shape), 0
        for kv_all in gathered:
            span = slice(first, first + kv_all.shape[1])
            o = attention(q, kv_all, first)
            part = jnp.einsum('btd,de->bte', o, w_out, preferred_element_type=jnp.float32)
            y = y.at[span].set((x[span].astype(jnp.float32) + part).astype(jnp.bfloat16))
            q, y = lax.optimization_barrier((q, y))
            first = span.stop
        return y

    return jax.shard_map(local_block, mesh=mesh, in_specs=(row_spec, P('data', 'cp'), rep_spec, rep_spec, rep_spec, rep_spec), out_specs=row_spec, check_vma=False)
```

time: 898 us -> 876 us (0.976)
  matrix products: 477 us -> 249 us
  Pallas kernels: 385 us -> 597 us
    pallas_call x2 -> x3, Pallas kernels: 111 us -> 352 us  [the longest x1 240 us: project_q(): pl.pallas_call(functools.partial(q_kernel, n_tiles), grid=(n_tiles + 1,),...]
    dot_general x1 -> x0, matrix products: 228 us -> none  [local_block(): jnp.einsum('bte,ed->btd', x, w_query, preferred_element_type=jnp.float32)]
    pallas_call x3, Pallas kernels: 274 us -> 244 us  [attention(): pl.pallas_call(functools.partial(attn_kernel, n_steps), grid=(n_steps + 1...]
  transfers between devices with their start and end apart: 3 -> 3, of which waited for: 0 -> 0; matrix products, arithmetic and copies ran while one was open for 43% -> 21% of each run, Pallas kernels for 28% -> 56%
where the time goes in v2:
time: 876 us; the launch traced here: 869 us
  Pallas kernels  597 us (68%)
  matrix products  249 us (28%)
  between operations  13.6 us (2%)
  other arithmetic  9.7 us (1%)
    dot_general x3, matrix products, local_block(): jnp.einsum('btd,de->bte', o, w_out, preferred_element_type=jnp.float32)  249 us
    pallas_call x3, Pallas kernels, attention(): pl.pallas_call(functools.partial(attn_kernel, n_steps), grid=(n_steps + 1...  244 us
    pallas_call x1, Pallas kernels, project_q(): pl.pallas_call(functools.partial(q_kernel, n_tiles), grid=(n_tiles + 1,),...  240 us
    pallas_call x2, Pallas kernels, project_kv(): pl.pallas_call(functools.partial(kv_kernel, chunks), grid=(total // ROWS,...  112 us
  transfers between devices with their start and end apart: 3, of which 0 were waited for; matrix products, arithmetic and copies ran while one was open for 21% of the time, Pallas kernels for 56%

profile of v2, /device:TPU:0, one launch (start us, length us, event | category | flops | bytes accessed | tf_op | source)
XLA Modules:
  0.0 869.4 jit_solution(5365268807439359985)
XLA Ops:
  6.5 0.0 all-gather.7.cloned.1.call-start
  6.5 0.1 compare_select_fusion
  6.6 0.7 convert_element_type.21
  7.4 8.9 %fusion.17 = (f32[16,256,128]{2,1,0:T(8,128)}, f32[16,256,128]{2,1,0:T(8,128)}) fusion(f32[128]{0:T(128)S(1)} %get-tuple-element.63, f32[128]{0:T(128)S(1)} %get-tuple-element.64, f32[16,256]{1,0:T(8,128)S(1)} %convert_element_type.21), kind=kLoop, calls=%fused_computation.14 | loop fusion | flops 1048576 | bytes 4211712 | tf_op jit(solution)/shard_map/mul | solution.py:31
  16.2 44.0 %kv_proj.2 = bf16[6,256,2048]{2,1,0:T(8,128)(2,1)} custom-call(bf16[16,256,5120]{2,1,0:T(8,128)(2,1)} %x_ref.3, bf16[5120,1024]{1,0:T(8,128)(2,1)} %wk_ref.3, bf16[5120,1024]{1,0:T(8,128)(2,1)} %wv_ref.3, f32[16,256,128]{2,1,0:T(8,128)} %get-tuple-element.62.cos_ref, f32[16,256,128]{2,1,0:T(8,128)} %get-tuple-element.61.sin_ref), custom_call_target="tpu_custom_call" | custom-call | flops 32212254720 | bytes 36700160 | tf_op jit(solution)/shard_map/kv_proj/pallas_call | solution.py:78
  60.3 0.0 all-gather.7.cloned.1.call-update
  60.3 0.0 all-gather.9.cloned.1.call-start
  60.4 68.1 %kv_proj.3 = (bf16[6,256,2048]{2,1,0:T(8,128)(2,1)}, bf16[4,256,2048]{2,1,0:T(8,128)(2,1)}) custom-call(bf16[16,256,5120]{2,1,0:T(8,128)(2,1)} %x_ref.3, bf16[5120,1024]{1,0:T(8,128)(2,1)} %wk_ref.3, bf16[5120,1024]{1,0:T(8,128)(2,1)} %wv_ref.3, f32[16,256,128]{2,1,0:T(8,128)} %get-tuple-element.62.cos_ref, f32[16,256,128]{2,1,0:T(8,128)} %get-tuple-element.61.sin_ref), custom_call_target="tpu_custom_call" | custom-call | flops 53687091200 | bytes 47185920 | tf_op jit(solution)/shard_map/kv_proj/pallas_call | solution.py:78
  128.5 0.0 all-gather.9.cloned.1.call-update
  128.5 0.0 all-gather.11.cloned.1.call-start
  128.5 0.7 all-gather.11.cloned.1.call-update
  129.2 239.9 %q_proj.1.q_ref = bf16[16,256,5120]{2,1,0:T(8,128)(2,1)} custom-call(bf16[16,256,5120]{2,1,0:T(8,128)(2,1)} %x_ref.3, bf16[5120,5120]{1,0:T(8,128)(2,1)} %w_ref.1, f32[16,256,128]{2,1,0:T(8,128)} %get-tuple-element.62.cos_ref, f32[16,256,128]{2,1,0:T(8,128)} %get-tuple-element.61.sin_ref), custom_call_target="tpu_custom_call" | custom-call | flops 214748364800 | bytes 136314880 | tf_op jit(solution)/shard_map/q_proj/pallas_call | solution.py:121
  369.1 0.0 all-gather.7.cloned.1.call-done
  369.1 90.9 %attn.3 = bf16[6,256,5120]{2,1,0:T(8,128)(2,1)} custom-call(bf16[16,256,5120]{2,1,0:T(8,128)(2,1)} %q_proj.1.q_ref, bf16[8,6,256,2048]{3,2,1,0:T(8,128)(2,1)} %bitcast.21, bf16[8,6,256,2048]{3,2,1,0:T(8,128)(2,1)} %bitcast.22), custom_call_target="tpu_custom_call" | custom-call | flops 34225520640 | bytes 81788928 | tf_op jit(solution)/shard_map/attn/pallas_call | solution.py:219
  460.0 92.3 %fusion.6 = bf16[16,256,5120]{2,1,0:T(8,128)(2,1)} fusion(bf16[16,256,5120]{2,1,0:T(8,128)(2,1)} %unset.1, bf16[16,256,5120]{2,1,0:T(8,128)(2,1)} %x_ref.3, bf16[6,256,5120]{2,1,0:T(8,128)(2,1)} %attn.3, bf16[5120,5120]{1,0:T(8,128)(2,1)} %param.17), kind=kOutput, calls=%fused_computation.9 | convolution fusion | flops 80554229760 | bytes 99614720 | tf_op jit(solution)/shard_map/btd,de->bte/dot_general | solution.py:269
  552.3 0.0 all-gather.9.cloned.1.call-done
  552.3 91.4 %attn.4 = bf16[6,256,5120]{2,1,0:T(8,128)(2,1)} custom-call(bf16[16,256,5120]{2,1,0:T(8,128)(2,1)} %q_proj.1.q_ref, bf16[8,6,256,2048]{3,2,1,0:T(8,128)(2,1)} %bitcast.23, bf16[8,6,256,2048]{3,2,1,0:T(8,128)(2,1)} %bitcast.24), custom_call_target="tpu_custom_call" | custom-call | flops 34225520640 | bytes 81788928 | tf_op jit(solution)/shard_map/attn/pallas_call | solution.py:219
  643.8 92.3 %fusion.7 = bf16[16,256,5120]{2,1,0:T(8,128)(2,1)} fusion(bf16[16,256,5120]{2,1,0:T(8,128)(2,1)} %fusion.6, bf16[16,256,5120]{2,1,0:T(8,128)(2,1)} %x_ref.3, bf16[6,256,5120]{2,1,0:T(8,128)(2,1)} %attn.4, bf16[5120,5120]{1,0:T(8,128)(2,1)} %param.17), kind=kOutput, calls=%fused_computation.10 | convolution fusion | flops 80554229760 | bytes 99614720 | tf_op jit(solution)/shard_map/btd,de->bte/dot_general | solution.py:269
  736.0 0.0 all-gather.11.cloned.1.call-done
  736.0 62.2 %attn.5 = bf16[4,256,5120]{2,1,0:T(8,128)(2,1)} custom-call(bf16[16,256,5120]{2,1,0:T(8,128)(2,1)} %q_proj.1.q_ref, bf16[8,4,256,2048]{3,2,1,0:T(8,128)(2,1)} %bitcast.25, bf16[8,4,256,2048]{3,2,1,0:T(8,128)(2,1)} %bitcast.26), custom_call_target="tpu_custom_call" | custom-call | flops 22817013760 | bytes 54525952 | tf_op jit(solution)/shard_map/attn/pallas_call | solution.py:219
  798.2 64.2 %fusion.14 = bf16[16,256,5120]{2,1,0:T(8,128)(2,1)} fusion(bf16[16,256,5120]{2,1,0:T(8,128)(2,1)} %fusion.7, bf16[4,256,5120]{2,1,0:T(8,128)(2,1)} %attn.5, bf16[5120,5120]{1,0:T(8,128)(2,1)} %param.17, bf16[16,256,5120]{2,1,0:T(8,128)(2,1)} %x_ref.3), kind=kOutput, calls=%fused_computation.11 | convolution fusion | flops 53702819840 | bytes 83886080 | tf_op jit(solution)/shard_map/btd,de->bte/dot_general | solution.py:269
  (2 shorter events, 0.0 us)
Async XLA Ops:
  6.5 362.6 %all-gather.7.cloned.1.call-start = ((), (), s32[]{:S(2)}) async-start(), calls=%async_computation | async-start | bytes 56623104 | tf_op jit(solution)/shard_map/all_gather | solution.py:262
  60.3 492.0 %all-gather.9.cloned.1.call-start = ((), (), s32[]{:S(2)}) async-start(), calls=%async_computation.1 | async-start | bytes 56623104 | tf_op jit(solution)/shard_map/all_gather | solution.py:262
  128.5 607.5 %all-gather.11.cloned.1.call-start = ((), (), s32[]{:S(2)}) async-start(), calls=%async_computation.2 | async-start | bytes 37748736 | tf_op jit(solution)/shard_map/all_gather | solution.py:262
Sparse Core Ops, SparseCore 0:
  60.4 229.4 all-gather.6
  291.7 226.6 all-gather.8
  520.2 155.2 all-gather.10
